TPU v7x, 32 devices: a whole 2x2x4 slice. The times are simulated.
32 devices in a mesh: dev: 4 (over y, x), ma: 8 (over z, core).
Axes of the slice: x: 2, y: 2, z: 4, core: 2. Of those that a mesh axis runs over, the one named last changes fastest.
Arguments:
- joined_weight: bfloat16 [8, 4096, 6144], P(None, 'dev', 'ma'), may hold values from -6 to 6
- norm_gain: float32 [8, 4096], P(None, 'ma'), may hold values from 0.5 to 1.5
- rotary_order: int32 [128], replicated, may hold values from 0 to 127, each once
Outputs:
- query_weight: bfloat16 [8, 4096, 4096], P(None, 'dev', 'ma')
- key_weight: bfloat16 [8, 1024, 4096], P(None, 'dev', 'ma')
- value_weight: bfloat16 [8, 1024, 4096], P(None, 'dev', 'ma')
- row_peak: float32 [8, 6144], P(None, 'dev')
Inputs may be any that keep to these rules, and one draw needn't show every extreme that they name: rotary_order holds every number of 0 to 127 exactly once.
All inputs are finite; a program needn't handle non-finite values.
Results may differ from a plain program's by a relative error of at most 0.0055.
Values may be sent and summed in bfloat16 or wider, within the bound.
A program may use at most 256 MiB of HBM per device.

v0:
```python
import jax
import jax.numpy as jnp
from jax import lax
from jax.sharding import PartitionSpec as P

HEADS = 32
KV_HEADS = 8
GROUP = 4


def arrange(stored):
    layer_count, row_count, column_count = stored.shape
    head_total = HEADS + 2 * KV_HEADS
    split = stored.reshape(layer_count, row_count, column_count // head_total, head_total)
    slots_query = split[..., :HEADS].reshape(layer_count, row_count, -1, KV_HEADS, GROUP)
    slots_key = split[..., HEADS : HEADS + KV_HEADS][..., None]
    slots_value = split[..., HEADS + KV_HEADS :][..., None]
    grouped = jnp.concatenate([slots_query, slots_key, slots_value], axis=4)
    return grouped


def settle(moved):
    return jnp.transpose(moved, (0, 3, 4, 2, 1))


def finish_tiles(canonical, gain_rows, rotary_order):
    layer_count = canonical.shape[0]
    column_count = canonical.shape[4]
    turned = jnp.take(canonical[:, :, : GROUP + 1], rotary_order, axis=3)
    complete = jnp.concatenate([turned, canonical[:, :, GROUP + 1 :]], axis=2)
    scaled = (complete.astype(jnp.float32) * gain_rows[:, None, None, None, :]).astype(jnp.bfloat16)
    query_rows = scaled[:, :, :GROUP].reshape(layer_count, -1, column_count)
    key_rows = scaled[:, :, GROUP].reshape(layer_count, -1, column_count)
    value_rows = scaled[:, :, GROUP + 1].reshape(layer_count, -1, column_count)
    local_peak = jnp.max(jnp.abs(scaled.astype(jnp.float32)), axis=4).reshape(layer_count, -1)
    return (query_rows, key_rows, value_rows, local_peak)


def shards(joined_weight, norm_gain, rotary_order):
    first_split, first_concat = (3, 1)
    second_split, second_concat = (1, 2)
    prepared = arrange(joined_weight)
    grouped = lax.all_to_all(
        prepared, "dev", split_axis=first_split, concat_axis=first_concat, tiled=True
    )
    moved = lax.all_to_all(
        grouped, "ma", split_axis=second_split, concat_axis=second_concat, tiled=True
    )
    query_rows, key_rows, value_rows, local_peak = finish_tiles(
        settle(moved), norm_gain, rotary_order
    )
    row_peak = lax.pmax(local_peak, "ma")
    return (query_rows, key_rows, value_rows, row_peak)


def solution(mesh):
    in_specs = (P(None, "dev", "ma"), P(None, "ma"), P())
    out_specs = (P(None, "dev", "ma"), P(None, "dev", "ma"), P(None, "dev", "ma"), P(None, "dev"))
    return jax.shard_map(shards, mesh=mesh, in_specs=in_specs, out_specs=out_specs, check_vma=False)
```

profile of v0, /device:TPU:0, one launch (start us, length us, event | category | flops | bytes accessed | tf_op | source)
XLA Modules:
  0.0 1059.1 jit_solution(12789976853737459264)
XLA Ops:
  0.6 16.6 %copy.54 = bf16[8,1024,768]{1,2,0:T(8,128)(2,1)} copy(bf16[8,1024,768]{2,1,0:T(8,128)(2,1)} %param.3) | data formatting | bytes 25165824 | tf_op args[0]
  17.3 2.7 slice_bitcast_fusion.1
  19.9 8.7 slice.34
  28.6 1.2 copy.56
  29.8 1.2 copy.57
  31.0 11.9 %copy.55 = bf16[8,1024,16,32]{1,2,3,0:T(8,128)(2,1)} copy(bf16[8,1024,16,32]{1,3,2,0:T(8,128)(2,1)} %slice.34) | data formatting | bytes 16777216 | tf_op jit(solution)/shard_map/slice | solution.py:15
  43.0 8.8 pad_maximum_fusion
  51.8 1.9 copy.58
  53.8 142.8 %all_to_all.36 = bf16[8,1024,16,8,6]{1,2,4,0,3:T(8,128)(2,1)S(1)} all-to-all(bf16[8,1024,16,8,6]{1,2,4,0,3:T(8,128)(2,1)S(1)} %copy.58), channel_id=1, replica_groups=mesh['dev'=4,'ma'=8] {'dev'}, dimensions={3} | all-to-all | bytes 25165824 | tf_op jit(solution)/shard_map/all_to_all | solution.py:43
  196.6 10.6 %copy.72 = bf16[8,1024,16,4,2,6]{1,3,2,5,4,0:T(4,128)(2,1)} copy(bf16[8,1024,16,4,2,6]{1,2,5,0,4,3:T(8,128)(2,1)S(1)} %bitcast.31) | data formatting | bytes 25165824 | tf_op jit(solution)/shard_map/all_to_all | solution.py:43
  207.2 92.5 %copy.68 = bf16[8,4,1024,16,2,6]{3,0,5,4,2,1:T(8,128)(2,1)} copy(bf16[8,4,1024,16,2,6]{2,1,3,5,4,0:T(4,128)(2,1)} %bitcast.28) | data formatting | bytes 25165824 | tf_op jit(solution)/shard_map/all_to_all | solution.py:43
  299.7 159.5 %reshape.39 = bf16[8,2,393216]{2,1,0:T(2,128)(2,1)} reshape(bf16[4096,2,6,8,16]{4,3,2,1,0:T(8,128)(2,1)} %bitcast.23) | data formatting | bytes 25165824
  459.3 0.0 copy-start.2
  459.3 5.3 all-to-all-start.1
  464.6 0.0 copy-done.2
  464.7 273.7 %all-to-all-done.1 = bf16[8,2,393216]{2,1,0:T(2,128)(2,1)} async-done(((bf16[8,2,393216]{2,1,0:T(2,128)(2,1)}), bf16[8,2,393216]{2,1,0:T(2,128)(2,1)}, u32[]{:S(2)}, u32[]{:S(2)}) %all-to-all-start.1) | async-done | bytes 12582944 | tf_op jit(solution)/shard_map/all_to_all | solution.py:46
  738.4 114.7 %reshape.40 = bf16[4096,2,6,8,16]{4,3,2,1,0:T(8,128)(2,1)} reshape(bf16[8,2,393216]{2,1,0:T(2,128)(2,1)} %all-to-all-done.1) | data formatting | bytes 25165824
  853.1 104.2 %copy.62 = bf16[8,512,8,16,2,6]{1,0,5,4,3,2:T(8,128)(2,1)} copy(bf16[8,512,8,16,2,6]{3,0,5,4,1,2:T(8,128)(2,1)} %bitcast.9) | data formatting | bytes 25165824 | tf_op jit(solution)/shard_map/all_to_all | solution.py:46
  957.3 9.0 slice.37
  966.3 1.8 slice.38
  968.0 8.8 copy.63
  976.9 11.7 %gather_fusion = bf16[128,8,2,5,512]{4,1,3,2,0:T(8,128)(2,1)} fusion(bf16[8,2,5,128,512]{4,0,3,2,1:T(8,128)(2,1)} %copy.63, s32[1024]{0:T(1024)S(1)} %pad_clamp_fusion), kind=kCustom, calls=%fused_computation | custom fusion | bytes 20972032 | tf_op jit(solution)/shard_map/jit(_take)/gather | solution.py:29
  988.5 5.8 select_bitcast_fusion
  994.3 6.6 abs_reduce_fusion
  1000.9 4.5 copy-done
  1005.5 0.5 fusion
  1006.0 8.3 slice.39
  1014.3 2.5 copy.65
  1016.8 2.5 copy.66
  1019.3 11.5 %copy.64 = bf16[8,2,4,128,512]{4,3,2,1,0:T(8,128)(2,1)} copy(bf16[8,2,4,128,512]{4,0,2,1,3:T(8,128)(2,1)} %slice.39) | data formatting | bytes 16777216 | tf_op jit(solution)/shard_map/slice | solution.py:32
  1030.8 0.3 copy.67
  1031.1 27.7 %pmax.7 = f32[8,1536]{1,0:T(8,128)} all-reduce(f32[8,1536]{1,0:T(8,128)S(1)} %bitcast.36), channel_id=1, replica_groups=mesh['dev'=4,'ma'=8] {'ma'}, use_global_device_ids=true, to_apply=%region_1.2 | all-reduce | flops 12288 | bytes 98304 | tf_op jit(solution)/shard_map/pmax | solution.py:52
  (6 shorter events, 0.0 us)
Async XLA Ops:
  459.3 5.4 copy-start.2
  459.3 279.1 %all-to-all-start.1 = ((bf16[8,2,393216]{2,1,0:T(2,128)(2,1)}), bf16[8,2,393216]{2,1,0:T(2,128)(2,1)}, u32[]{:S(2)}, u32[]{:S(2)}) async-start(bf16[8,2,393216]{2,1,0:T(2,128)(2,1)} %reshape.39), calls=%async_computation.1 | async-start | bytes 25165824 | tf_op jit(solution)/shard_map/all_to_all | solution.py:46
  988.5 5.8 copy-start.1
  1000.9 4.6 copy-start
where the time goes:
time: 1070 us; the launch traced here: 1060 us
  local copies, waits for them, and re-layouts  587 us (55%)
  waiting for transfers between devices  274 us (26%)
  blocking collectives  171 us (16%)
  other arithmetic  21.2 us (2%)
    unnamed x9, local copies, waits for them, and re-layouts  295 us
    all_to_all x1, waiting for transfers between devices, shards(): lax.all_to_all(grouped, 'ma', split_axis=second_split, concat_axis=second...  274 us
    all_to_all x1, blocking collectives, shards(): lax.all_to_all(prepared, 'dev', split_axis=first_split, concat_axis=first...  143 us
    all_to_all x1, local copies, waits for them, and re-layouts, shards(): lax.all_to_all(grouped, 'ma', split_axis=second_split, concat_axis=second...  104 us
    all_to_all x2, local copies, waits for them, and re-layouts, shards(): lax.all_to_all(prepared, 'dev', split_axis=first_split, concat_axis=first...  103 us
    pmax x1, blocking collectives, shards(): row_peak = lax.pmax(local_peak, 'ma')  27.7 us
  transfers between devices with their start and end apart: 1, of which 1 were waited for; matrix products, arithmetic and copies ran while one was open for 0% of the time, Pallas kernels for 0%

commit v1 on v0

v1 whole, which is shorter than its diff:
```python
import jax
import jax.numpy as jnp
from jax import lax
from jax.experimental import pallas as pl
from jax.experimental.pallas import tpu as pltpu
from jax.sharding import PartitionSpec as P

HEADS = 32
KV_HEADS = 8
GROUP = 4
SLOTS = GROUP + 2


def pack_kernel(order_ref, stored_ref, out_ref):
    rows = lax.dot_general(
        order_ref[...],
        stored_ref[0],
        (((1,), (1,)), ((), ())),
        preferred_element_type=jnp.float32,
    ).astype(jnp.bfloat16)
    out_ref[...] = rows.reshape(out_ref.shape)


def pack(joined, order, parts, halves):
    layers, features, columns = joined.shape
    width = features // halves
    rows = columns // parts
    return pl.pallas_call(
        pack_kernel,
        grid=(layers, halves),
        in_specs=[
            pl.BlockSpec((columns, columns), lambda l, h: (0, 0)),
            pl.BlockSpec((1, width, columns), lambda l, h: (l, h, 0)),
        ],
        out_specs=pl.BlockSpec((parts, 1, 1, rows, width), lambda l, h: (0, h, l, 0, 0)),
        out_shape=jax.ShapeDtypeStruct((parts, halves, layers, rows, width), joined.dtype),
    )(order, joined)


def finish_kernel(turn_ref, gain_ref, moved_ref, query_ref, key_ref, value_ref, peak_ref):
    gain = gain_ref[0]
    head_dim = turn_ref.shape[0]
    for slot in range(SLOTS):
        tile = moved_ref[:, 0, 0, slot].reshape(head_dim, moved_ref.shape[5])
        if slot <= GROUP:
            tile = jnp.dot(turn_ref[...], tile, preferred_element_type=jnp.float32)
        scaled = (tile.astype(jnp.float32) * gain).astype(jnp.bfloat16)
        if slot < GROUP:
            query_ref[0, slot * head_dim : (slot + 1) * head_dim, :] = scaled
        elif slot == GROUP:
            key_ref[0] = scaled
        else:
            value_ref[0] = scaled
        size = jnp.abs(scaled.astype(jnp.float32))
        step = min(128, size.shape[1])
        top = size[:, :step]
        for start in range(step, size.shape[1], step):
            top = jnp.maximum(top, size[:, start : start + step])
        peak_ref[0, 0, slot : slot + 1, :] = jnp.max(top.T, axis=0, keepdims=True)


def finish(moved, gain, turn):
    sources, layers, groups, slots, piece, width = moved.shape
    head_dim = sources * piece
    return pl.pallas_call(
        finish_kernel,
        grid=(layers, groups),
        in_specs=[
            pl.BlockSpec((head_dim, head_dim), lambda l, g: (0, 0)),
            pl.BlockSpec((1, 1, width), lambda l, g: (l, 0, 0)),
            pl.BlockSpec((sources, 1, 1, slots, piece, width), lambda l, g: (0, l, g, 0, 0, 0)),
        ],
        out_specs=[
            pl.BlockSpec((1, GROUP * head_dim, width), lambda l, g: (l, g, 0)),
            pl.BlockSpec((1, head_dim, width), lambda l, g: (l, g, 0)),
            pl.BlockSpec((1, head_dim, width), lambda l, g: (l, g, 0)),
            pl.BlockSpec((1, 1, slots, head_dim), lambda l, g: (l, g, 0, 0)),
        ],
        out_shape=[
            jax.ShapeDtypeStruct((layers, groups * GROUP * head_dim, width), moved.dtype),
            jax.ShapeDtypeStruct((layers, groups * head_dim, width), moved.dtype),
            jax.ShapeDtypeStruct((layers, groups * head_dim, width), moved.dtype),
            jax.ShapeDtypeStruct((layers, groups, slots, head_dim), jnp.float32),
        ],
    )(turn, gain[:, None, :], moved)


def column_order(columns):
    head_total = HEADS + 2 * KV_HEADS
    piece = columns // head_total
    row = jnp.arange(columns)
    group = row // (SLOTS * piece)
    slot = (row // piece) % SLOTS
    dim = row % piece
    head = jnp.where(
        slot < GROUP,
        group * GROUP + slot,
        jnp.where(slot == GROUP, HEADS + group, HEADS + KV_HEADS + group),
    )
    source = dim * head_total + head
    return (source[:, None] == jnp.arange(columns)[None, :]).astype(jnp.bfloat16)


def solution(mesh):
    parts = mesh.shape["dev"]
    sources = mesh.shape["ma"]

    def shards(joined_weight, norm_gain, rotary_order):
        layers, features, columns = joined_weight.shape
        width = norm_gain.shape[1]
        halves = features // width
        piece = columns // (HEADS + 2 * KV_HEADS)
        packed = pack(joined_weight, column_order(columns), parts, halves)
        grouped = lax.all_to_all(packed, "dev", split_axis=0, concat_axis=0, tiled=True)
        grouped = grouped.reshape(sources, layers, columns // parts, width)
        moved = lax.all_to_all(grouped, "ma", split_axis=0, concat_axis=0, tiled=True)
        moved = moved.reshape(sources, layers, KV_HEADS // parts, SLOTS, piece, width)
        head_dim = rotary_order.shape[0]
        turn = (rotary_order[:, None] == jnp.arange(head_dim)[None, :]).astype(jnp.bfloat16)
        query_rows, key_rows, value_rows, peak = finish(moved, norm_gain, turn)
        row_peak = lax.pmax(peak.reshape(layers, -1), "ma")
        return (query_rows, key_rows, value_rows, row_peak)

    in_specs = (P(None, "dev", "ma"), P(None, "ma"), P())
    out_specs = (P(None, "dev", "ma"), P(None, "dev", "ma"), P(None, "dev", "ma"), P(None, "dev"))
    return jax.shard_map(shards, mesh=mesh, in_specs=in_specs, out_specs=out_specs, check_vma=False)
```

time: 1070 us -> 496 us (0.46)
  local copies, waits for them, and re-layouts: 587 us -> 1.49 us
  Pallas kernels: 0 us -> 35.9 us
  other arithmetic: 21.2 us -> 1.99 us
    unnamed x9 -> x4, local copies, waits for them, and re-layouts: 295 us -> 0.01 us
    all_to_all x3 -> x0, local copies, waits for them, and re-layouts: 207 us -> none  [the longest x1 104 us: shards(): lax.all_to_all(grouped, 'ma', split_axis=second_split, concat_axis=second...]
    slice x10 -> x0, local copies, waits for them, and re-layouts: 65.5 us -> none  [the longest x2 20.6 us: arrange(): split[..., :HEADS].reshape(layer_count, row_count, -1, KV_HEADS, GROUP)]
    pallas_call x0 -> x2, Pallas kernels: none -> 35.9 us  [the longest x1 20.2 us: pack(): pl.pallas_call(pack_kernel, grid=(layers, halves), in_specs=[pl.BlockSpec...]
    gather x1 -> x0, local copies, waits for them, and re-layouts: 11.7 us -> none  [finish_tiles(): turned = jnp.take(canonical[:, :, :GROUP + 1], rotary_order, axis=3)]
where the time goes in v1:
time: 496 us; the launch traced here: 494 us
  waiting for transfers between devices  272 us (55%)
  blocking collectives  176 us (35%)
  Pallas kernels  35.9 us (7%)
  starting transfers between devices  5.49 us (1%)
    all_to_all x1, waiting for transfers between devices, shards(): lax.all_to_all(grouped, 'ma', split_axis=0, concat_axis=0, tiled=True)  272 us
    all_to_all x1, blocking collectives, shards(): lax.all_to_all(packed, 'dev', split_axis=0, concat_axis=0, tiled=True)  149 us
    pmax x1, blocking collectives, shards(): row_peak = lax.pmax(peak.reshape(layers, -1), 'ma')  27.7 us
    pallas_call x1, Pallas kernels, pack(): pl.pallas_call(pack_kernel, grid=(layers, halves), in_specs=[pl.BlockSpec...  20.2 us
    pallas_call x1, Pallas kernels, finish(): pl.pallas_call(finish_kernel, grid=(layers, groups), in_specs=[pl.BlockSp...  15.7 us
  transfers between devices with their start and end apart: 1, of which 1 were waited for; matrix products, arithmetic and copies ran while one was open for 0% of the time, Pallas kernels for 0%

profile of v1, /device:TPU:0, one launch (start us, length us, event | category | flops | bytes accessed | tf_op | source)
XLA Modules:
  0.0 494.3 jit_solution(11854181961330282274)
XLA Ops:
  0.6 1.3 fusion.order_ref
  1.9 20.2 %shard_map.66 = bf16[4,2,8,192,512]{4,3,2,1,0:T(8,128)(2,1)} custom-call(bf16[768,768]{1,0:T(8,128)(2,1)} %fusion.order_ref, bf16[8,1024,768]{2,1,0:T(8,128)(2,1)} %stored_ref.1), custom_call_target="tpu_custom_call" | custom-call | tf_op jit(solution)/shard_map/pallas_call | solution.py:28
  22.1 148.6 %all_to_all.10 = bf16[4,2,8,192,512]{4,3,2,1,0:T(8,128)(2,1)} all-to-all(bf16[4,2,8,192,512]{4,3,2,1,0:T(8,128)(2,1)} %shard_map.66), channel_id=1, replica_groups=mesh['dev'=4,'ma'=8] {'dev'}, dimensions={0} | all-to-all | bytes 25165824 | tf_op jit(solution)/shard_map/all_to_all | solution.py:114
  170.7 0.0 copy-start
  170.7 0.0 copy-start.1
  170.7 5.5 %all-to-all-start.1 = ((bf16[8,8,192,512]{3,2,1,0:T(8,128)(2,1)}), bf16[8,8,192,512]{3,2,1,0:T(8,128)(2,1)}, u32[]{:S(2)}, u32[]{:S(2)}) async-start(bf16[8,8,192,512]{3,2,1,0:T(8,128)(2,1)} %bitcast.2), calls=%async_computation.1 | async-start | bytes 25165824 | tf_op jit(solution)/shard_map/all_to_all | solution.py:116
  176.2 0.0 copy-done
  176.2 0.6 broadcast_in_dim.2.gain_ref
  176.9 0.0 copy-done.1
  176.9 0.7 fusion.1.turn_ref
  177.6 272.4 %all-to-all-done.1 = bf16[8,8,192,512]{3,2,1,0:T(8,128)(2,1)} async-done(((bf16[8,8,192,512]{3,2,1,0:T(8,128)(2,1)}), bf16[8,8,192,512]{3,2,1,0:T(8,128)(2,1)}, u32[]{:S(2)}, u32[]{:S(2)}) %all-to-all-start.1) | async-done | bytes 12582944 | tf_op jit(solution)/shard_map/all_to_all | solution.py:116
  450.0 15.7 %shard_map.67 = (bf16[8,1024,512]{2,1,0:T(8,128)(2,1)}, bf16[8,256,512]{2,1,0:T(8,128)(2,1)}, bf16[8,256,512]{2,1,0:T(8,128)(2,1)}, f32[8,2,6,128]{3,2,1,0:T(8,128)}) custom-call(bf16[128,128]{1,0:T(8,128)(2,1)} %fusion.1.turn_ref, f32[8,1,512]{2,1,0:T(1,128)} %broadcast_in_dim.2.gain_ref, bf16[8,8,2,6,16,512]{5,4,3,2,1,0:T(8,128)(2,1)} %bitcast.1.moved_ref), custom_call_target="tpu_custom_call" | custom-call | tf_op jit(solution)/shard_map/pallas_call | solution.py:65
  465.7 0.9 reshape.64
  466.6 27.7 %pmax.7 = f32[8,1536]{1,0:T(8,128)} all-reduce(f32[8,1536]{1,0:T(8,128)S(1)} %reshape.64), channel_id=1, replica_groups=mesh['dev'=4,'ma'=8] {'ma'}, use_global_device_ids=true, to_apply=%region_0.1 | all-reduce | flops 12288 | bytes 98304 | tf_op jit(solution)/shard_map/pmax | solution.py:121
  (1 shorter events, 0.0 us)
Async XLA Ops:
  170.7 5.5 %copy-start = (f32[8,512]{1,0:T(8,128)S(1)}, f32[8,512]{1,0:T(8,128)}, u32[]{:S(2)}) copy-start(f32[8,512]{1,0:T(8,128)} %param.4) | copy-start | bytes 49156
  170.7 6.1 %copy-start.1 = (s32[128]{0:T(128)S(1)}, s32[128]{0:T(128)}, u32[]{:S(2)}) copy-start(s32[128]{0:T(128)} %param.5) | copy-start | bytes 1540
  170.7 279.2 %all-to-all-start.1 = ((bf16[8,8,192,512]{3,2,1,0:T(8,128)(2,1)}), bf16[8,8,192,512]{3,2,1,0:T(8,128)(2,1)}, u32[]{:S(2)}, u32[]{:S(2)}) async-start(bf16[8,8,192,512]{3,2,1,0:T(8,128)(2,1)} %bitcast.2), calls=%async_computation.1 | async-start | bytes 25165824 | tf_op jit(solution)/shard_map/all_to_all | solution.py:116
